TPU v7x, 32 devices: a whole 2x2x4 slice. The times are simulated.
32 devices in a mesh: pts: 8 (over z, core), head: 4 (over y, x).
Axes of the slice: x: 2, y: 2, z: 4, core: 2. Of those that a mesh axis runs over, the one named last changes fastest.
Arguments:
- points: bfloat16 [73728, 128], P('pts')
- counts: int32 [8], P('pts'), may hold values from 1 to 9216, 55296 in all
- ln1_gain: float32 [2, 128], replicated, may hold values from 0.5 to 1.5
- ln1_bias: float32 [2, 128], replicated, may hold values from -1.5 to 1.5
- w_in: bfloat16 [2, 128, 128], P(None, None, 'head'), may hold values from -0.5 to 0.5
- w_fx: bfloat16 [2, 128, 128], P(None, None, 'head'), may hold values from -0.5 to 0.5
- w_slice: bfloat16 [2, 32, 32], replicated
- temper: float32 [2, 4], replicated, may hold values from 0.5 to 2
- query_weight: bfloat16 [2, 32, 32], replicated
- key_weight: bfloat16 [2, 32, 32], replicated, may hold values from -1 to 1
- value_weight: bfloat16 [2, 32, 32], replicated, may hold values from -1 to 1
- w_out: bfloat16 [2, 128, 128], P(None, 'head'), may hold values from -1 to 1
- b_out: float32 [2, 128], replicated, may hold values from -1.5 to 1.5
- ln2_gain: float32 [2, 128], replicated, may hold values from 0.5 to 1.5
- ln2_bias: float32 [2, 128], replicated, may hold values from -1.5 to 1.5
- w_up: bfloat16 [2, 128, 512], replicated, may hold values from -0.5 to 0.5
- w_down: bfloat16 [2, 512, 128], replicated, may hold values from -0.25 to 0.25
Outputs:
- features: bfloat16 [73728, 128], P(('pts', 'head'))
Inputs may be any that keep to these rules, and one draw needn't show every extreme that they name: counts[i] live points fill the first slots of shard i; at least one shard is full; they sum to 55296.
All inputs are finite; a program needn't handle non-finite values.
Results may differ from a plain program's by a relative error of at most 0.014.
Values may be sent and summed in bfloat16 or wider, within the bound.
A program may use at most 128 MiB of HBM per device.

v0:
```python
import jax
import jax.numpy as jnp
from jax import lax
from jax.sharding import PartitionSpec as P

DH = 32
M = 32


def layer_norm(value, gain, bias):
    mean = jnp.mean(value, axis=-1, keepdims=True)
    centred = value - mean
    var = jnp.mean(centred * centred, axis=-1, keepdims=True)
    return centred * lax.rsqrt(var + 1e-05) * gain + bias


def slice_attention(token_rows, query_weight, key_weight, value_weight):
    head_parts = lax.Precision.HIGHEST
    query_rows = jnp.einsum(
        "aur,rz->auz", token_rows, query_weight.astype(jnp.float32), precision=head_parts
    )
    slice_keys = jnp.einsum(
        "aur,rz->auz", token_rows, key_weight.astype(jnp.float32), precision=head_parts
    )
    slice_values = jnp.einsum(
        "aur,rz->auz", token_rows, value_weight.astype(jnp.float32), precision=head_parts
    )
    scores = jnp.einsum("hme,hke->hmk", query_rows, slice_keys, precision=head_parts) * DH ** (-0.5)
    attn = jax.nn.softmax(scores, axis=-1)
    return jnp.einsum("hmk,hke->hme", attn, slice_values, precision=head_parts).astype(jnp.bfloat16)


def body(
    points,
    counts,
    ln1_gain,
    ln1_bias,
    w_in,
    w_fx,
    w_slice,
    temper,
    query_weight,
    key_weight,
    value_weight,
    w_out,
    b_out,
    ln2_gain,
    ln2_bias,
    w_up,
    w_down,
):
    groups = lax.axis_size("head")
    rows = points.shape[0] // groups
    first_row = lax.axis_index("head") * rows
    layers = w_in.shape[0]
    full_in = lax.all_gather(w_in, "head", axis=2, tiled=True)
    full_fx = lax.all_gather(w_fx, "head", axis=2, tiled=True)
    full_out = lax.all_gather(w_out, "head", axis=1, tiled=True)
    heads = full_in.shape[2] // DH
    live = (first_row + jnp.arange(rows, dtype=jnp.int32) < counts[0]).astype(jnp.float32)
    current = lax.dynamic_slice_in_dim(points, first_row, rows, 0)
    for layer_index in range(layers):
        normed = layer_norm(
            current.astype(jnp.float32), ln1_gain[layer_index], ln1_bias[layer_index]
        ).astype(jnp.bfloat16)
        mid = jnp.dot(normed, full_in[layer_index], preferred_element_type=jnp.float32).astype(
            jnp.bfloat16
        )
        feats = jnp.dot(normed, full_fx[layer_index], preferred_element_type=jnp.float32).astype(
            jnp.bfloat16
        )
        spread = jnp.kron(jnp.eye(heads, dtype=jnp.bfloat16), w_slice[layer_index])
        logits = jnp.dot(mid, spread, preferred_element_type=jnp.float32)
        logits = logits.reshape(rows, heads, M) / temper[layer_index][None, :, None]
        weights = jax.nn.softmax(logits, axis=-1) * live[:, None, None]
        half_weights = weights.astype(jnp.bfloat16).reshape(rows, heads * M)
        total = jnp.sum(weights, axis=0)
        square = jnp.einsum("rs,rl->sl", half_weights, feats, preferred_element_type=jnp.float32)
        square = square.reshape(heads, M, heads, DH)
        numerator = jnp.stack([square[h, :, h, :] for h in range(heads)])
        numerator, total = lax.psum((numerator, total), ("pts", "head"))
        token_rows = numerator / jnp.maximum(total, 1.0)[..., None]
        mixed_token = slice_attention(
            token_rows,
            query_weight[layer_index],
            key_weight[layer_index],
            value_weight[layer_index],
        )
        wide = (
            jnp.einsum(
                "hmv,hvc->hmc",
                mixed_token,
                full_out[layer_index].reshape(heads, DH, -1),
                preferred_element_type=jnp.float32,
            )
            .astype(jnp.bfloat16)
            .reshape(heads * M, -1)
        )
        projected = jnp.dot(half_weights, wide, preferred_element_type=jnp.float32)
        after = current.astype(jnp.float32) + projected + b_out[layer_index]
        normed2 = layer_norm(after, ln2_gain[layer_index], ln2_bias[layer_index]).astype(
            jnp.bfloat16
        )
        upper = jax.nn.gelu(
            jnp.dot(normed2, w_up[layer_index], preferred_element_type=jnp.float32)
        ).astype(jnp.bfloat16)
        current = (
            after + jnp.dot(upper, w_down[layer_index], preferred_element_type=jnp.float32)
        ).astype(jnp.bfloat16)
    return current


def solution(mesh):
    placed = (
        P("pts", None),
        P("pts"),
        P(),
        P(),
        P(None, None, "head"),
        P(None, None, "head"),
        P(),
        P(),
        P(),
        P(),
        P(),
        P(None, "head", None),
        P(),
        P(),
        P(),
        P(),
        P(),
    )
    return jax.shard_map(
        body, mesh=mesh, in_specs=placed, out_specs=P(("pts", "head"), None), check_vma=False
    )
```

profile of v0, /device:TPU:0, one launch (start us, length us, event | category | flops | bytes accessed | tf_op | source)
XLA Modules:
  0.0 157.5 jit_solution(5383199505180625222)
XLA Ops:
  0.0 1.7 %copy-done = bf16[9216,128]{1,0:T(8,128)(2,1)S(1)} copy-done((bf16[9216,128]{1,0:T(8,128)(2,1)S(1)}, bf16[9216,128]{1,0:T(8,128)(2,1)}, u32[]{:S(2)}) %copy-start) | copy-done | bytes 2359320
  3.5 0.8 broadcast_multiply_fusion
  4.4 9.7 %all_gather.9 = bf16[2,128,128]{1,2,0:T(8,128)(2,1)S(1)} all-gather(bf16[2,128,32]{1,2,0:T(8,128)(2,1)S(1)} %copy-done.10), channel_id=1, replica_groups=mesh['pts'=8,'head'=4] {'head'}, dimensions={2}, use_global_device_ids=true | all-gather | bytes 81920 | tf_op jit(solution)/shard_map/all_gather | solution.py:56
  14.2 1.9 %fusion.122 = (f32[2304,4]{0,1:T(4,128)S(1)}, f32[2304,4,32]{0,2,1:T(8,128)}) fusion(bf16[4,32,128]{2,1,0:T(8,128)(2,1)S(1)} %bitcast.209, f32[4]{0:T(128)S(1)} %get-tuple-element.28, bf16[2,128,128]{1,2,0:T(8,128)(2,1)S(1)} %all_gather.9, bf16[2304,128]{0,1:T(8,128)(2,1)S(1)} %copy.26, f32[128]{0:T(128)S(1)} %get-tuple-element.34, ...), kind=kOutput, calls=%fused_computation.175 | convolution fusion | flops 153944096 | bytes 1897984 | tf_op jit(solution)/shard_map/sub | solution.py:75
  16.7 1.6 %fusion.57 = f32[4,32]{1,0:T(4,128)S(1)} fusion(f32[2304]{0:T(1024)S(1)} %fusion.83, f32[2304,4,32]{0,2,1:T(8,128)} %get-tuple-element.36, f32[2304,4]{0,1:T(4,128)S(1)} %get-tuple-element.35), kind=kLoop, calls=%fused_computation.77 | loop fusion | flops 884608 | bytes 1226240 | tf_op jit(solution)/shard_map/reduce_sum | solution.py:77
  18.3 8.2 %all_gather.10 = bf16[2,128,128]{1,2,0:T(8,128)(2,1)S(1)} all-gather(bf16[2,128,32]{1,2,0:T(8,128)(2,1)S(1)} %copy-done.11), channel_id=1, replica_groups=mesh['pts'=8,'head'=4] {'head'}, dimensions={2}, use_global_device_ids=true | all-gather | bytes 81920 | tf_op jit(solution)/shard_map/all_gather | solution.py:57
  27.7 40.2 %all-reduce.1 = (f32[4,32,32]{2,1,0:T(8,128)S(1)}, f32[4,32]{1,0:T(4,128)S(1)}) all-reduce(f32[4,32,32]{2,1,0:T(8,128)S(1)} %pad_maximum_fusion, f32[4,32]{1,0:T(4,128)S(1)} %fusion.57), channel_id=1, replica_groups=mesh['pts'=8,'head'=4] {'pts','head'}, use_global_device_ids=true, to_apply=%region_4.5 | all-reduce | flops 4224 | bytes 33792 | tf_op jit(solution)/shard_map/psum | solution.py:81
  69.3 9.0 %all_gather.11 = bf16[2,128,128]{2,1,0:T(8,128)(2,1)S(1)} all-gather(bf16[2,32,128]{2,1,0:T(8,128)(2,1)S(1)} %copy-done.12), channel_id=1, replica_groups=mesh['pts'=8,'head'=4] {'head'}, dimensions={1}, use_global_device_ids=true | all-gather | bytes 81920 | tf_op jit(solution)/shard_map/all_gather | solution.py:58
  79.4 2.8 %fusion.126 = (f32[2304]{0:T(1024)S(1)}, f32[2304,128]{0,1:T(8,128)}) fusion(f32[128]{0:T(128)S(1)} %get-tuple-element.26, bf16[4,32,32]{2,1,0:T(8,128)(2,1)S(1)} %convolution_convert_fusion.7, bf16[4,32,128]{2,1,0:T(8,128)(2,1)S(1)} %bitcast.212, f32[2304]{0:T(1024)S(1)} %fusion.83, f32[2304,4,32]{0,2,1:T(8,128)} %get-tuple-element.36, ...), kind=kOutput, calls=%fused_computation.177 | convolution fusion | flops 78624512 | bytes 3045888 | tf_op jit(solution)/shard_map/dot_general | solution.py:99
  82.2 1.4 multiply_reduce_fusion.2
  84.8 4.6 %fusion.127 = (f32[2304]{0:T(1024)}, f32[2304,128]{0,1:T(8,128)S(1)}) fusion(f32[2304,128]{0,1:T(8,128)} %get-tuple-element.40, bf16[2,512,128]{2,1,0:T(8,128)(2,1)} %param.33, f32[128]{0:T(128)} %get-tuple-element.24, f32[128]{0:T(128)} %get-tuple-element.51, f32[2304]{0:T(1024)} %add_rsqrt_fusion.2, f32[2304]{0:T(1024)} %copy-done.8, ...), kind=kOutput, calls=%fused_computation.178 | convolution fusion | flops 617248512 | bytes 3835904 | tf_op jit(solution)/shard_map/dot_general | solution.py:108
  90.3 1.2 add_convert_fusion.1
  91.5 1.6 %mul.210 = bf16[128,128]{0,1:T(8,128)(2,1)} reshape(bf16[4,32,4,32]{1,0,3,2:T(4,128)(2,1)} %get-tuple-element.29) | data formatting | bytes 65536 | tf_op jit(solution)/shard_map/jit(kron)/mul | solution.py:72
  93.1 3.4 %fusion.130 = (f32[2304,4]{0,1:T(4,128)}, f32[2304,4,32]{0,2,1:T(8,128)}) fusion(bf16[4,32,128]{2,1,0:T(8,128)(2,1)} %bitcast.210, bf16[2304,128]{0,1:T(8,128)(2,1)} %add_convert_fusion.1, f32[4]{0:T(128)S(1)} %get-tuple-element.27, bf16[2,128,128]{1,2,0:T(8,128)(2,1)} %copy-done.7), kind=kOutput, calls=%fused_computation.179 | convolution fusion | flops 152174624 | bytes 1871888 | tf_op jit(solution)/shard_map/sub | solution.py:75
  96.5 1.6 %fusion.59 = f32[4,32]{1,0:T(4,128)S(1)} fusion(f32[2304]{0:T(1024)S(1)} %fusion.83, f32[2304,4,32]{0,2,1:T(8,128)} %get-tuple-element.44, f32[2304,4]{0,1:T(4,128)} %get-tuple-element.43), kind=kLoop, calls=%fused_computation.79 | loop fusion | flops 884608 | bytes 1226240 | tf_op jit(solution)/shard_map/reduce_sum | solution.py:77
  99.7 40.3 %all-reduce = (f32[4,32,32]{2,1,0:T(8,128)}, f32[4,32]{1,0:T(4,128)}) all-reduce(f32[4,32,32]{2,1,0:T(8,128)} %pad_maximum_fusion.1, f32[4,32]{1,0:T(4,128)S(1)} %fusion.59), channel_id=1, replica_groups=mesh['pts'=8,'head'=4] {'pts','head'}, use_global_device_ids=true, to_apply=%region_15.16 | all-reduce | flops 4224 | bytes 33792 | tf_op jit(solution)/shard_map/psum | solution.py:81
  140.7 1.1 fusion.86
  141.8 1.1 fusion.88
  143.1 1.1 fusion.84
  144.2 0.9 convolution_convert_fusion.5
  145.2 3.4 %fusion.132 = (f32[2304]{0:T(1024)}, f32[2304,128]{0,1:T(8,128)}) fusion(f32[128]{0:T(128)} %get-tuple-element.25, f32[2304,128]{0,1:T(8,128)S(1)} %get-tuple-element.42, bf16[4,32,32]{2,1,0:T(8,128)(2,1)} %convolution_convert_fusion.5, bf16[4,32,128]{2,1,0:T(8,128)(2,1)} %bitcast.211, f32[2304]{0:T(1024)S(1)} %fusion.83, ...), kind=kOutput, calls=%fused_computation.181 | convolution fusion | flops 78329600 | bytes 3635712 | tf_op jit(solution)/shard_map/dot_general | solution.py:99
  149.4 1.4 multiply_reduce_fusion
  151.4 4.0 %fusion.27 = bf16[2304,128]{0,1:T(8,128)(2,1)} fusion(f32[2304,128]{0,1:T(8,128)S(1)} %copy-done.4, f32[128]{0:T(128)S(1)} %copy-done.22, f32[128]{0:T(128)} %get-tuple-element.52, f32[2304]{0:T(1024)} %add_rsqrt_fusion, f32[2304]{0:T(1024)S(1)} %broadcast_multiply_fusion.2, bf16[2,512,128]{2,1,0:T(8,128)(2,1)} %param.33, bf16[2,128,512]{2,1,0:T(8,128)(2,1)} %param.32), kind=kOutput, calls=%fused_computation.35 | convolution fusion | flops 616660992 | bytes 3236864 | tf_op jit(solution)/shard_map/dot_general | solution.py:108
  155.4 2.1 %copy.22 = bf16[2304,128]{1,0:T(8,128)(2,1)} copy(bf16[2304,128]{0,1:T(8,128)(2,1)} %fusion.27) | data formatting | bytes 1179648 | tf_op jit(solution)/shard_map/convert_element_type | solution.py:109
  (93 shorter events, 11.4 us)
Async XLA Ops:
  0.0 1.7 %copy-start = (bf16[9216,128]{1,0:T(8,128)(2,1)S(1)}, bf16[9216,128]{1,0:T(8,128)(2,1)}, u32[]{:S(2)}) copy-start(bf16[9216,128]{1,0:T(8,128)(2,1)} %param.17) | copy-start | bytes 7077892
  1.7 1.6 copy-start.13
  2.0 2.4 %copy-start.10 = (bf16[2,128,32]{1,2,0:T(8,128)(2,1)S(1)}, bf16[2,128,32]{1,2,0:T(8,128)(2,1)}, u32[]{:S(2)}) copy-start(bf16[2,128,32]{1,2,0:T(8,128)(2,1)} %param.21) | copy-start | bytes 49156
  2.0 12.1 %copy-start.16 = (f32[2,4]{1,0:T(2,128)S(1)}, f32[2,4]{1,0:T(2,128)}, u32[]{:S(2)}) copy-start(f32[2,4]{1,0:T(2,128)} %param.24) | copy-start | bytes 100
  14.1 1.9 %copy-start.7 = (bf16[2,128,128]{1,2,0:T(8,128)(2,1)}, bf16[2,128,128]{1,2,0:T(8,128)(2,1)S(1)}, u32[]{:S(2)}) copy-start(bf16[2,128,128]{1,2,0:T(8,128)(2,1)S(1)} %all_gather.9) | copy-start | bytes 196612
  16.0 2.3 %copy-start.11 = (bf16[2,128,32]{1,2,0:T(8,128)(2,1)S(1)}, bf16[2,128,32]{1,2,0:T(8,128)(2,1)}, u32[]{:S(2)}) copy-start(bf16[2,128,32]{1,2,0:T(8,128)(2,1)} %param.22) | copy-start | bytes 49156
  16.7 10.3 %copy-start.2 = (f32[2304,4,32]{0,2,1:T(8,128)S(1)}, f32[2304,4,32]{0,2,1:T(8,128)}, u32[]{:S(2)}) copy-start(f32[2304,4,32]{0,2,1:T(8,128)} %get-tuple-element.36) | copy-start | bytes 3538948
  26.5 1.1 copy-start.5
  27.0 40.9 %copy-start.23 = (bf16[2,32,32]{2,1,0:T(8,128)(2,1)S(1)}, bf16[2,32,32]{2,1,0:T(8,128)(2,1)}, u32[]{:S(2)}) copy-start(bf16[2,32,32]{2,1,0:T(8,128)(2,1)} %param.26) | copy-start | bytes 12292
  27.0 41.2 %copy-start.24 = (bf16[2,32,32]{2,1,0:T(8,128)(2,1)S(1)}, bf16[2,32,32]{2,1,0:T(8,128)(2,1)}, u32[]{:S(2)}) copy-start(bf16[2,32,32]{2,1,0:T(8,128)(2,1)} %param.25) | copy-start | bytes 12292
  27.0 41.7 %copy-start.25 = (bf16[2,32,32]{2,1,0:T(8,128)(2,1)S(1)}, bf16[2,32,32]{2,1,0:T(8,128)(2,1)}, u32[]{:S(2)}) copy-start(bf16[2,32,32]{2,1,0:T(8,128)(2,1)} %param.27) | copy-start | bytes 12292
  27.6 41.6 %copy-start.12 = (bf16[2,32,128]{2,1,0:T(8,128)(2,1)S(1)}, bf16[2,32,128]{2,1,0:T(8,128)(2,1)}, u32[]{:S(2)}) copy-start(bf16[2,32,128]{2,1,0:T(8,128)(2,1)} %param.28) | copy-start | bytes 49156
  27.6 51.2 %copy-start.17 = (f32[2,128]{1,0:T(2,128)S(1)}, f32[2,128]{1,0:T(2,128)}, u32[]{:S(2)}) copy-start(f32[2,128]{1,0:T(2,128)} %param.29) | copy-start | bytes 3076
  82.2 2.1 %copy-start.20 = (f32[2,128]{1,0:T(2,128)S(1)}, f32[2,128]{1,0:T(2,128)}, u32[]{:S(2)}) copy-start(f32[2,128]{1,0:T(2,128)} %param.31) | copy-start | bytes 3076
  82.2 2.1 %copy-start.21 = (f32[2,128]{1,0:T(2,128)S(1)}, f32[2,128]{1,0:T(2,128)}, u32[]{:S(2)}) copy-start(f32[2,128]{1,0:T(2,128)} %param.30) | copy-start | bytes 3076
  82.2 2.7 %copy-start.8 = (f32[2304]{0:T(1024)}, f32[2304]{0:T(1024)S(1)}, u32[]{:S(2)}) copy-start(f32[2304]{0:T(1024)S(1)} %broadcast_multiply_fusion.4) | copy-start | bytes 27652
  89.4 0.9 copy-start.14
  89.4 0.9 copy-start.15
  96.5 1.6 %copy-start.1 = (bf16[2304,128]{0,1:T(8,128)(2,1)S(1)}, bf16[2304,128]{0,1:T(8,128)(2,1)}, u32[]{:S(2)}) copy-start(bf16[2304,128]{0,1:T(8,128)(2,1)} %add_convert_fusion.1) | copy-start | bytes 1769476
  96.5 1.6 %copy-start.6 = (bf16[2,128,128]{1,2,0:T(8,128)(2,1)S(1)}, bf16[2,128,128]{1,2,0:T(8,128)(2,1)}, u32[]{:S(2)}) copy-start(bf16[2,128,128]{1,2,0:T(8,128)(2,1)} %copy-done.5) | copy-start | bytes 196612
  96.5 2.0 %copy-start.3 = (f32[2304,4,32]{0,2,1:T(8,128)S(1)}, f32[2304,4,32]{0,2,1:T(8,128)}, u32[]{:S(2)}) copy-start(f32[2304,4,32]{0,2,1:T(8,128)} %get-tuple-element.44) | copy-start | bytes 3538948
  96.5 2.0 %copy-start.9 = (f32[2304,4]{0,1:T(4,128)S(1)}, f32[2304,4]{0,1:T(4,128)}, u32[]{:S(2)}) copy-start(f32[2304,4]{0,1:T(4,128)} %get-tuple-element.43) | copy-start | bytes 110596
  148.6 2.8 %copy-start.4 = (f32[2304,128]{0,1:T(8,128)S(1)}, f32[2304,128]{0,1:T(8,128)}, u32[]{:S(2)}) copy-start(f32[2304,128]{0,1:T(8,128)} %get-tuple-element.48) | copy-start | bytes 3538948
  148.6 2.8 %copy-start.22 = (f32[128]{0:T(128)S(1)}, f32[128]{0:T(128)}, u32[]{:S(2)}) copy-start(f32[128]{0:T(128)} %get-tuple-element.23) | copy-start | bytes 1540
  (2 other events, 1.4 us)
where the time goes:
time: 159 us; the launch traced here: 158 us
  blocking collectives  107 us (67%)
  matrix products  27.6 us (17%)
  other arithmetic  12.6 us (8%)
  local copies, waits for them, and re-layouts  8.79 us (6%)
    psum x2, blocking collectives, body(): numerator, total = lax.psum((numerator, total), ('pts', 'head'))  80.5 us
    all_gather x1, blocking collectives, body(): full_in = lax.all_gather(w_in, 'head', axis=2, tiled=True)  9.72 us
    all_gather x1, blocking collectives, body(): full_out = lax.all_gather(w_out, 'head', axis=1, tiled=True)  9 us
    dot_general x2, matrix products, body(): jnp.dot(upper, w_down[layer_index], preferred_element_type=jnp.float32)  8.51 us
    all_gather x1, blocking collectives, body(): full_fx = lax.all_gather(w_fx, 'head', axis=2, tiled=True)  8.21 us
    dot_general x2, matrix products, body(): projected = jnp.dot(half_weights, wide, preferred_element_type=jnp.float32)  6.22 us
    sub x2, matrix products, body(): weights = jax.nn.softmax(logits, axis=-1) * live[:, None, None]  5.29 us
    reduce_sum x2, other arithmetic, body(): total = jnp.sum(weights, axis=0)  3.22 us

commit v1 on v0

--- a/solution.py
+++ b/solution.py
@@ -5,6 +5,12 @@
 
 DH = 32
 M = 32
+
+
+def move_the_links(message, mesh_ax, along_axis):
+    for at in (mesh_ax, along_axis):
+        message = jax.lax.psum(message, axis_name=at)
+    return message
 
 
 def layer_norm(value, gain, bias):
@@ -78,7 +84,7 @@
         square = jnp.einsum("rs,rl->sl", half_weights, feats, preferred_element_type=jnp.float32)
         square = square.reshape(heads, M, heads, DH)
         numerator = jnp.stack([square[h, :, h, :] for h in range(heads)])
-        numerator, total = lax.psum((numerator, total), ("pts", "head"))
+        numerator, total = move_the_links((numerator, total), "head", "pts")
         token_rows = numerator / jnp.maximum(total, 1.0)[..., None]
         mixed_token = slice_attention(
             token_rows,

time: 159 us -> 164 us (1.031)
  blocking collectives: 107 us -> 114 us
    psum x2 -> x4, blocking collectives: 80.5 us -> 88.7 us  [move_the_links(): message = jax.lax.psum(message, axis_name=at)]
    all_gather x1, blocking collectives: 9 us -> 7.34 us  [body(): full_out = lax.all_gather(w_out, 'head', axis=1, tiled=True)]
where the time goes in v1:
time: 164 us; the launch traced here: 163 us
  blocking collectives  114 us (70%)
  matrix products  27.6 us (17%)
  other arithmetic  12 us (7%)
  local copies, waits for them, and re-layouts  8.79 us (5%)
    psum x4, blocking collectives, move_the_links(): message = jax.lax.psum(message, axis_name=at)  88.7 us
    all_gather x1, blocking collectives, body(): full_in = lax.all_gather(w_in, 'head', axis=2, tiled=True)  9.72 us
    dot_general x2, matrix products, body(): jnp.dot(upper, w_down[layer_index], preferred_element_type=jnp.float32)  8.51 us
    all_gather x1, blocking collectives, body(): full_fx = lax.all_gather(w_fx, 'head', axis=2, tiled=True)  8.21 us
    all_gather x1, blocking collectives, body(): full_out = lax.all_gather(w_out, 'head', axis=1, tiled=True)  7.34 us
    dot_general x2, matrix products, body(): projected = jnp.dot(half_weights, wide, preferred_element_type=jnp.float32)  6.22 us
    sub x2, matrix products, body(): weights = jax.nn.softmax(logits, axis=-1) * live[:, None, None]  5.29 us

profile of v1, /device:TPU:0, one launch (start us, length us, event | category | flops | bytes accessed | tf_op | source)
XLA Modules:
  0.0 163.4 jit_solution(9723353268955519072)
XLA Ops:
  0.0 1.7 %copy-done = bf16[9216,128]{1,0:T(8,128)(2,1)S(1)} copy-done((bf16[9216,128]{1,0:T(8,128)(2,1)S(1)}, bf16[9216,128]{1,0:T(8,128)(2,1)}, u32[]{:S(2)}) %copy-start) | copy-done | bytes 2359320
  4.4 9.7 %all_gather.9 = bf16[2,128,128]{1,2,0:T(8,128)(2,1)S(1)} all-gather(bf16[2,128,32]{1,2,0:T(8,128)(2,1)S(1)} %copy-done.10), channel_id=1, replica_groups=mesh['pts'=8,'head'=4] {'head'}, dimensions={2}, use_global_device_ids=true | all-gather | bytes 81920 | tf_op jit(solution)/shard_map/all_gather | solution.py:62
  14.2 1.9 %fusion.122 = (f32[2304,4]{0,1:T(4,128)S(1)}, f32[2304,4,32]{0,2,1:T(8,128)}) fusion(bf16[4,32,128]{2,1,0:T(8,128)(2,1)S(1)} %bitcast.209, f32[4]{0:T(128)S(1)} %get-tuple-element.32, bf16[2,128,128]{1,2,0:T(8,128)(2,1)S(1)} %all_gather.9, bf16[2304,128]{0,1:T(8,128)(2,1)S(1)} %copy.26, f32[128]{0:T(128)S(1)} %get-tuple-element.38, ...), kind=kOutput, calls=%fused_computation.175 | convolution fusion | flops 153944096 | bytes 1897984 | tf_op jit(solution)/shard_map/sub | solution.py:81
  16.7 1.6 fusion.57
  18.3 8.2 %all_gather.10 = bf16[2,128,128]{1,2,0:T(8,128)(2,1)S(1)} all-gather(bf16[2,128,32]{1,2,0:T(8,128)(2,1)S(1)} %copy-done.11), channel_id=1, replica_groups=mesh['pts'=8,'head'=4] {'head'}, dimensions={2}, use_global_device_ids=true | all-gather | bytes 81920 | tf_op jit(solution)/shard_map/all_gather | solution.py:63
  27.7 16.5 %all-reduce.3 = (f32[4,32,32]{2,1,0:T(8,128)S(1)}, f32[4,32]{1,0:T(4,128)S(1)}) all-reduce(f32[4,32,32]{2,1,0:T(8,128)S(1)} %pad_maximum_fusion, f32[4,32]{1,0:T(4,128)S(1)} %fusion.57), channel_id=1, replica_groups=mesh['pts'=8,'head'=4] {'head'}, use_global_device_ids=true, to_apply=%region_4.5 | all-reduce | flops 4224 | bytes 33792 | tf_op jit(solution)/shard_map/psum | solution.py:12
  44.2 26.8 %all-reduce.1 = (f32[4,32,32]{2,1,0:T(8,128)S(1)}, f32[4,32]{1,0:T(4,128)S(1)}) all-reduce(f32[4,32,32]{2,1,0:T(8,128)S(1)} %get-tuple-element.11, f32[4,32]{1,0:T(4,128)S(1)} %get-tuple-element.12), channel_id=1, replica_groups=mesh['pts'=8,'head'=4] {'pts'}, use_global_device_ids=true, to_apply=%region_5.6 | all-reduce | flops 4224 | bytes 33792 | tf_op jit(solution)/shard_map/psum | solution.py:12
  72.4 7.3 %all_gather.11 = bf16[2,128,128]{2,1,0:T(8,128)(2,1)S(1)} all-gather(bf16[2,32,128]{2,1,0:T(8,128)(2,1)S(1)} %copy-done.12), channel_id=1, replica_groups=mesh['pts'=8,'head'=4] {'head'}, dimensions={1}, use_global_device_ids=true | all-gather | bytes 81920 | tf_op jit(solution)/shard_map/all_gather | solution.py:64
  80.9 2.8 %fusion.126 = (f32[2304]{0:T(1024)S(1)}, f32[2304,128]{0,1:T(8,128)}) fusion(f32[128]{0:T(128)S(1)} %get-tuple-element.30, bf16[4,32,32]{2,1,0:T(8,128)(2,1)S(1)} %convolution_convert_fusion.7, bf16[4,32,128]{2,1,0:T(8,128)(2,1)S(1)} %bitcast.212, f32[2304]{0:T(1024)S(1)} %fusion.83, f32[2304,4,32]{0,2,1:T(8,128)} %get-tuple-element.40, ...), kind=kOutput, calls=%fused_computation.177 | convolution fusion | flops 78624512 | bytes 3045888 | tf_op jit(solution)/shard_map/dot_general | solution.py:105
  83.7 1.4 multiply_reduce_fusion.2
  86.3 4.5 %fusion.127 = (f32[2304]{0:T(1024)}, f32[2304,128]{0,1:T(8,128)S(1)}) fusion(f32[2304,128]{0,1:T(8,128)} %get-tuple-element.44, bf16[2,512,128]{2,1,0:T(8,128)(2,1)} %param.33, f32[128]{0:T(128)} %get-tuple-element.28, f32[128]{0:T(128)} %get-tuple-element.55, f32[2304]{0:T(1024)} %add_rsqrt_fusion.2, f32[2304]{0:T(1024)} %copy-done.8, ...), kind=kOutput, calls=%fused_computation.178 | convolution fusion | flops 617248512 | bytes 3835904 | tf_op jit(solution)/shard_map/dot_general | solution.py:114
  91.8 1.2 add_convert_fusion.1
  93.0 1.6 %mul.210 = bf16[128,128]{0,1:T(8,128)(2,1)} reshape(bf16[4,32,4,32]{1,0,3,2:T(4,128)(2,1)} %get-tuple-element.33) | data formatting | bytes 65536 | tf_op jit(solution)/shard_map/jit(kron)/mul | solution.py:78
  94.6 3.4 %fusion.130 = (f32[2304,4]{0,1:T(4,128)}, f32[2304,4,32]{0,2,1:T(8,128)}) fusion(bf16[4,32,128]{2,1,0:T(8,128)(2,1)} %bitcast.210, bf16[2304,128]{0,1:T(8,128)(2,1)} %add_convert_fusion.1, f32[4]{0:T(128)S(1)} %get-tuple-element.31, bf16[2,128,128]{1,2,0:T(8,128)(2,1)} %copy-done.7), kind=kOutput, calls=%fused_computation.179 | convolution fusion | flops 152174624 | bytes 1871888 | tf_op jit(solution)/shard_map/sub | solution.py:81
  98.0 1.6 fusion.59
  101.2 17.4 %all-reduce.2 = (f32[4,32,32]{2,1,0:T(8,128)}, f32[4,32]{1,0:T(4,128)}) all-reduce(f32[4,32,32]{2,1,0:T(8,128)} %pad_maximum_fusion.1, f32[4,32]{1,0:T(4,128)S(1)} %fusion.59), channel_id=1, replica_groups=mesh['pts'=8,'head'=4] {'head'}, use_global_device_ids=true, to_apply=%region_17.18 | all-reduce | flops 4224 | bytes 33792 | tf_op jit(solution)/shard_map/psum | solution.py:12
  118.6 28.0 %all-reduce = (f32[4,32,32]{2,1,0:T(8,128)}, f32[4,32]{1,0:T(4,128)S(1)}) all-reduce(f32[4,32,32]{2,1,0:T(8,128)} %get-tuple-element.9, f32[4,32]{1,0:T(4,128)} %get-tuple-element.10), channel_id=1, replica_groups=mesh['pts'=8,'head'=4] {'pts'}, use_global_device_ids=true, to_apply=%region_18.19 | all-reduce | flops 4224 | bytes 33792 | tf_op jit(solution)/shard_map/psum | solution.py:12
  146.6 1.1 fusion.86
  147.7 1.1 fusion.88
  149.1 1.1 fusion.84
  151.1 3.4 %fusion.132 = (f32[2304]{0:T(1024)}, f32[2304,128]{0,1:T(8,128)}) fusion(f32[128]{0:T(128)} %get-tuple-element.29, f32[2304,128]{0,1:T(8,128)S(1)} %get-tuple-element.46, bf16[4,32,32]{2,1,0:T(8,128)(2,1)} %convolution_convert_fusion.5, bf16[4,32,128]{2,1,0:T(8,128)(2,1)} %bitcast.211, f32[2304]{0:T(1024)S(1)} %fusion.83, ...), kind=kOutput, calls=%fused_computation.181 | convolution fusion | flops 78329600 | bytes 3635712 | tf_op jit(solution)/shard_map/dot_general | solution.py:105
  155.3 1.4 multiply_reduce_fusion
  157.4 4.0 %fusion.27 = bf16[2304,128]{0,1:T(8,128)(2,1)} fusion(f32[2304,128]{0,1:T(8,128)S(1)} %copy-done.4, f32[128]{0:T(128)S(1)} %copy-done.22, f32[128]{0:T(128)} %get-tuple-element.56, f32[2304]{0:T(1024)} %add_rsqrt_fusion, f32[2304]{0:T(1024)S(1)} %broadcast_multiply_fusion.2, bf16[2,512,128]{2,1,0:T(8,128)(2,1)} %param.33, bf16[2,128,512]{2,1,0:T(8,128)(2,1)} %param.32), kind=kOutput, calls=%fused_computation.35 | convolution fusion | flops 616660992 | bytes 3236864 | tf_op jit(solution)/shard_map/dot_general | solution.py:114
  161.3 2.1 %copy.22 = bf16[2304,128]{1,0:T(8,128)(2,1)} copy(bf16[2304,128]{0,1:T(8,128)(2,1)} %fusion.27) | data formatting | bytes 1179648 | tf_op jit(solution)/shard_map/convert_element_type | solution.py:115
  (95 shorter events, 12.4 us)
Async XLA Ops:
  0.0 1.7 %copy-start = (bf16[9216,128]{1,0:T(8,128)(2,1)S(1)}, bf16[9216,128]{1,0:T(8,128)(2,1)}, u32[]{:S(2)}) copy-start(bf16[9216,128]{1,0:T(8,128)(2,1)} %param.17) | copy-start | bytes 7077892
  1.7 1.6 copy-start.13
  2.0 2.4 %copy-start.10 = (bf16[2,128,32]{1,2,0:T(8,128)(2,1)S(1)}, bf16[2,128,32]{1,2,0:T(8,128)(2,1)}, u32[]{:S(2)}) copy-start(bf16[2,128,32]{1,2,0:T(8,128)(2,1)} %param.21) | copy-start | bytes 49156
  2.0 12.1 %copy-start.16 = (f32[2,4]{1,0:T(2,128)S(1)}, f32[2,4]{1,0:T(2,128)}, u32[]{:S(2)}) copy-start(f32[2,4]{1,0:T(2,128)} %param.24) | copy-start | bytes 100
  14.1 1.9 %copy-start.7 = (bf16[2,128,128]{1,2,0:T(8,128)(2,1)}, bf16[2,128,128]{1,2,0:T(8,128)(2,1)S(1)}, u32[]{:S(2)}) copy-start(bf16[2,128,128]{1,2,0:T(8,128)(2,1)S(1)} %all_gather.9) | copy-start | bytes 196612
  16.0 2.3 %copy-start.11 = (bf16[2,128,32]{1,2,0:T(8,128)(2,1)S(1)}, bf16[2,128,32]{1,2,0:T(8,128)(2,1)}, u32[]{:S(2)}) copy-start(bf16[2,128,32]{1,2,0:T(8,128)(2,1)} %param.22) | copy-start | bytes 49156
  16.7 10.3 %copy-start.2 = (f32[2304,4,32]{0,2,1:T(8,128)S(1)}, f32[2304,4,32]{0,2,1:T(8,128)}, u32[]{:S(2)}) copy-start(f32[2304,4,32]{0,2,1:T(8,128)} %get-tuple-element.40) | copy-start | bytes 3538948
  26.5 1.1 copy-start.5
  27.0 44.1 %copy-start.23 = (bf16[2,32,32]{2,1,0:T(8,128)(2,1)S(1)}, bf16[2,32,32]{2,1,0:T(8,128)(2,1)}, u32[]{:S(2)}) copy-start(bf16[2,32,32]{2,1,0:T(8,128)(2,1)} %param.26) | copy-start | bytes 12292
  27.0 44.3 %copy-start.24 = (bf16[2,32,32]{2,1,0:T(8,128)(2,1)S(1)}, bf16[2,32,32]{2,1,0:T(8,128)(2,1)}, u32[]{:S(2)}) copy-start(bf16[2,32,32]{2,1,0:T(8,128)(2,1)} %param.25) | copy-start | bytes 12292
  27.0 44.8 %copy-start.25 = (bf16[2,32,32]{2,1,0:T(8,128)(2,1)S(1)}, bf16[2,32,32]{2,1,0:T(8,128)(2,1)}, u32[]{:S(2)}) copy-start(bf16[2,32,32]{2,1,0:T(8,128)(2,1)} %param.27) | copy-start | bytes 12292
  27.6 44.8 %copy-start.12 = (bf16[2,32,128]{2,1,0:T(8,128)(2,1)S(1)}, bf16[2,32,128]{2,1,0:T(8,128)(2,1)}, u32[]{:S(2)}) copy-start(bf16[2,32,128]{2,1,0:T(8,128)(2,1)} %param.28) | copy-start | bytes 49156
  27.6 52.7 %copy-start.17 = (f32[2,128]{1,0:T(2,128)S(1)}, f32[2,128]{1,0:T(2,128)}, u32[]{:S(2)}) copy-start(f32[2,128]{1,0:T(2,128)} %param.29) | copy-start | bytes 3076
  83.7 2.1 %copy-start.20 = (f32[2,128]{1,0:T(2,128)S(1)}, f32[2,128]{1,0:T(2,128)}, u32[]{:S(2)}) copy-start(f32[2,128]{1,0:T(2,128)} %param.31) | copy-start | bytes 3076
  83.7 2.1 %copy-start.21 = (f32[2,128]{1,0:T(2,128)S(1)}, f32[2,128]{1,0:T(2,128)}, u32[]{:S(2)}) copy-start(f32[2,128]{1,0:T(2,128)} %param.30) | copy-start | bytes 3076
  83.7 2.7 %copy-start.8 = (f32[2304]{0:T(1024)}, f32[2304]{0:T(1024)S(1)}, u32[]{:S(2)}) copy-start(f32[2304]{0:T(1024)S(1)} %broadcast_multiply_fusion.4) | copy-start | bytes 27652
  90.9 0.9 copy-start.14
  90.9 0.9 copy-start.15
  98.0 1.6 %copy-start.1 = (bf16[2304,128]{0,1:T(8,128)(2,1)S(1)}, bf16[2304,128]{0,1:T(8,128)(2,1)}, u32[]{:S(2)}) copy-start(bf16[2304,128]{0,1:T(8,128)(2,1)} %add_convert_fusion.1) | copy-start | bytes 1769476
  98.0 1.6 %copy-start.6 = (bf16[2,128,128]{1,2,0:T(8,128)(2,1)S(1)}, bf16[2,128,128]{1,2,0:T(8,128)(2,1)}, u32[]{:S(2)}) copy-start(bf16[2,128,128]{1,2,0:T(8,128)(2,1)} %copy-done.5) | copy-start | bytes 196612
  98.0 2.0 %copy-start.3 = (f32[2304,4,32]{0,2,1:T(8,128)S(1)}, f32[2304,4,32]{0,2,1:T(8,128)}, u32[]{:S(2)}) copy-start(f32[2304,4,32]{0,2,1:T(8,128)} %get-tuple-element.48) | copy-start | bytes 3538948
  98.0 2.0 %copy-start.9 = (f32[2304,4]{0,1:T(4,128)S(1)}, f32[2304,4]{0,1:T(4,128)}, u32[]{:S(2)}) copy-start(f32[2304,4]{0,1:T(4,128)} %get-tuple-element.47) | copy-start | bytes 110596
  154.5 2.8 %copy-start.4 = (f32[2304,128]{0,1:T(8,128)S(1)}, f32[2304,128]{0,1:T(8,128)}, u32[]{:S(2)}) copy-start(f32[2304,128]{0,1:T(8,128)} %get-tuple-element.52) | copy-start | bytes 3538948
  154.5 2.8 %copy-start.22 = (f32[128]{0:T(128)S(1)}, f32[128]{0:T(128)}, u32[]{:S(2)}) copy-start(f32[128]{0:T(128)} %get-tuple-element.27) | copy-start | bytes 1540
  (2 other events, 1.4 us)
